TPU v7x, 32 devices: a whole 2x2x4 slice. The times are simulated.
32 devices in a mesh: dp: 16 (over z, x, core), mp: 2 (over y).
Axes of the slice: x: 2, y: 2, z: 4, core: 2. Of those that a mesh axis runs over, the one named last changes fastest.
Arguments:
- ranges: bfloat16 [512, 2652], P(('dp', 'mp')), may hold values from 0.0099487305 to 1
- board: int32 [512, 5], P(('dp', 'mp')), may hold values from 0 to 51, as said below
- targets: bfloat16 [512, 2652], P(('dp', 'mp')), may hold values from -6 to 6
- w_in: bfloat16 [1536, 2704], P(('mp', 'dp')), may hold values from -0.34570312 to 0.34570312
- w_out: bfloat16 [1536, 2652], P(('mp', 'dp')), may hold values from -0.3046875 to 0.3046875
Outputs:
- predicted: bfloat16 [512, 2652], P(('dp', 'mp'))
- update_in: float32 [1536, 2704], P(('mp', 'dp'))
- update_out: float32 [1536, 2652], P(('mp', 'dp'))
- loss: float32 [], replicated
Inputs may be any that keep to these rules, and one draw needn't show every extreme that they name: `board`: each row holds 5 different cards.
All inputs are finite; a program needn't handle non-finite values.
Results may differ from a plain program's by a relative error of at most 0.014.
Values may be sent and summed in bfloat16 or wider, within the bound.
No kernel may reach another device: no remote copies, remote signals or barrier semaphores. Data moves between devices by JAX's collectives and lax.ppermute only.
A program may use at most 64 MiB of HBM per device.

v0:
```python
import jax
import jax.numpy as jnp
from jax import lax
from jax.sharding import PartitionSpec as P

CARDS = 52
HIDDEN_SIZE = 1536


def huber_terms(error_value):
    magnitude = jnp.abs(error_value)
    return jnp.where(magnitude <= 1.0, 0.5 * error_value * error_value, magnitude - 0.5)


def build_features(all_ranges, all_board, card_count):
    card_ids = jnp.arange(card_count, dtype=jnp.int32)
    onehot_board = jnp.sum(
        (all_board[:, :, None] == card_ids[None, None, :]).astype(jnp.float32), axis=1
    ).astype(jnp.bfloat16)
    return jnp.concatenate([all_ranges, onehot_board], axis=1)


def right_product(left_side, right_block):
    return lax.dot_general(
        left_side, right_block, (((1,), (1,)), ((), ())), preferred_element_type=jnp.float32
    )


def left_product(left_side, right_side):
    return lax.dot_general(
        left_side, right_side, (((0,), (0,)), ((), ())), preferred_element_type=jnp.float32
    )


def body(ranges, board, targets, w_in, w_out):
    mp_count = lax.axis_size("mp")
    dp_count = lax.axis_size("dp")
    stored_rows = ranges.shape[0]
    value_width = w_out.shape[1]
    all_ranges, all_board = (
        lax.all_gather(ranges, "mp", axis=0, tiled=True),
        lax.all_gather(board, "mp", axis=0, tiled=True),
    )
    features = build_features(all_ranges, all_board, CARDS)
    local_in = lax.all_gather(w_in, "dp", axis=0, tiled=True)
    preact = right_product(features, local_in)
    hidden = jax.nn.gelu(preact).astype(jnp.bfloat16)
    local_out = lax.all_gather(w_out, "dp", axis=0, tiled=True)
    partial_value = jnp.dot(hidden, local_out, preferred_element_type=jnp.float32)
    stacked = partial_value.astype(jnp.bfloat16).reshape(mp_count, stored_rows, value_width)
    received = lax.all_to_all(stacked, "mp", split_axis=0, concat_axis=0, tiled=True)
    summed = jnp.sum(received.astype(jnp.float32), axis=0)
    error_value = summed - targets.astype(jnp.float32)
    own_grad = jnp.clip(error_value, -1.0, 1.0).astype(jnp.bfloat16)
    out_grad = lax.all_gather(own_grad, "mp", axis=0, tiled=True)
    predicted = summed.astype(jnp.bfloat16)
    loss_part = jnp.sum(huber_terms(error_value))
    loss_total = lax.psum(loss_part, ("dp", "mp"))
    grad_out = lax.psum_scatter(
        left_product(hidden, out_grad), "dp", scatter_dimension=0, tiled=True
    )
    back_out = lax.all_gather(w_out, "dp", axis=0, tiled=True)
    hidden_grad = right_product(out_grad, back_out)
    unused_value, gelu_back = jax.vjp(jax.nn.gelu, preact)
    preact_grad = gelu_back(hidden_grad)[0].astype(jnp.bfloat16)
    grad_in = lax.psum_scatter(
        left_product(preact_grad, features), "dp", scatter_dimension=0, tiled=True
    )
    square_part = jnp.sum(grad_in * grad_in) + jnp.sum(grad_out * grad_out)
    square_total = lax.psum(square_part, ("dp", "mp"))
    count_params = HIDDEN_SIZE * (w_in.shape[1] + value_width)
    scale = lax.rsqrt(square_total / count_params + 1e-06)
    loss = loss_total / (stored_rows * mp_count * dp_count * value_width)
    return (predicted, grad_in * scale, grad_out * scale, loss)


def solution(mesh):
    in_specs = (
        P(("dp", "mp"), None),
        P(("dp", "mp"), None),
        P(("dp", "mp"), None),
        P(("mp", "dp"), None),
        P(("mp", "dp"), None),
    )
    out_specs = (P(("dp", "mp"), None), P(("mp", "dp"), None), P(("mp", "dp"), None), P())
    return jax.shard_map(body, mesh=mesh, in_specs=in_specs, out_specs=out_specs, check_vma=False)
```

profile of v0, /device:TPU:0, one launch (start us, length us, event | category | flops | bytes accessed | tf_op | source)
XLA Modules:
  0.0 402.8 jit_solution(9901448083366208325)
XLA Ops:
  7.2 0.0 all-gather.4.cloned.1.call-start
  7.2 0.7 all-gather.4.cloned.1.call-update
  7.9 0.0 all-gather.6.cloned.1.call-start
  7.9 0.7 all-gather.6.cloned.1.call-update
  8.6 0.0 reduce-scatter.5.cloned.1.call-start
  8.7 5.5 %all-gather = s32[2,16,5]{1,2,0:T(8,128)S(1)} all-gather(s32[1,16,5]{1,2,0:T(8,128)} %bitcast.10), channel_id=1, replica_groups=mesh['dp'=16,'mp'=2] {'mp'}, dimensions={0}, use_global_device_ids=true | all-gather | bytes 960 | tf_op jit(solution)/shard_map/all_gather | solution.py:42
  14.2 0.1 reshape.14
  14.3 5.4 %all_gather.16 = bf16[32,2652]{1,0:T(8,128)(2,1)S(1)} all-gather(bf16[16,2652]{1,0:T(8,128)(2,1)} %param.5), channel_id=1, replica_groups=mesh['dp'=16,'mp'=2] {'mp'}, dimensions={0}, use_global_device_ids=true | all-gather | bytes 254592 | tf_op jit(solution)/shard_map/all_gather | solution.py:41
  19.7 0.1 convert_reduce_fusion.1
  19.7 0.0 copy-start
  19.8 44.3 %all-gather.4.cloned.1.call-done = bf16[768,2704]{1,0:T(8,128)(2,1)} async-done(((bf16[48,2704]{1,0:T(8,128)(2,1)}), bf16[768,2704]{1,0:T(8,128)(2,1)}) %all-gather.4.cloned.1.call-update) | async-done | bytes 4153360 | tf_op jit(solution)/shard_map/all_gather | solution.py:45
  64.1 3.6 fusion.3
  67.6 47.4 %all-gather.6.cloned.1.call-done = bf16[768,2652]{1,0:T(8,128)(2,1)} async-done(((bf16[48,2652]{1,0:T(8,128)(2,1)}), bf16[768,2652]{1,0:T(8,128)(2,1)}) %all-gather.6.cloned.1.call-update) | async-done | bytes 4073488 | tf_op jit(solution)/shard_map/all_gather | solution.py:48
  115.1 3.0 convolution_convert_fusion
  118.0 7.2 %all_to_all.5 = bf16[2,16,2652]{2,1,0:T(8,128)(2,1)S(1)} all-to-all(bf16[2,16,2652]{2,1,0:T(8,128)(2,1)S(1)} %bitcast.9), channel_id=1, replica_groups=mesh['dp'=16,'mp'=2] {'mp'}, dimensions={0} | all-to-all | bytes 339456 | tf_op jit(solution)/shard_map/all_to_all | solution.py:51
  125.3 0.0 copy-done
  125.3 1.3 fusion.1
  126.6 5.1 %all_gather.20 = bf16[32,2652]{1,0:T(8,128)(2,1)S(1)} all-gather(bf16[16,2652]{1,0:T(8,128)(2,1)S(1)} %get-tuple-element.7), channel_id=1, replica_groups=mesh['dp'=16,'mp'=2] {'mp'}, dimensions={0}, use_global_device_ids=true | all-gather | bytes 254592 | tf_op jit(solution)/shard_map/all_gather | solution.py:55
  131.8 4.5 %fusion.26 = f32[768,2652]{1,0:T(8,128)} fusion(bf16[32,2652]{1,0:T(8,128)(2,1)S(1)} %all_gather.20, f32[32,768]{1,0:T(8,128)S(1)} %fusion.3), kind=kOutput, calls=%fused_computation.40 | convolution fusion | flops 130572288 | bytes 8414976 | tf_op jit(solution)/shard_map/dot_general | solution.py:30
  136.2 0.0 reduce-scatter.5.cloned.1.call-update
  136.2 0.0 reduce-scatter.3.cloned.1.call-start
  136.3 9.1 %fusion.2 = f32[768,2704]{1,0:T(8,128)} fusion(bf16[32,52]{1,0:T(8,128)(2,1)S(1)} %convert_reduce_fusion.1, bf16[32,2652]{1,0:T(8,128)(2,1)S(1)} %all_gather.16, f32[32,768]{1,0:T(8,128)S(1)} %fusion.3, bf16[32,2652]{1,0:T(8,128)(2,1)S(1)} %all_gather.20, bf16[768,2652]{1,0:T(8,128)(2,1)} %all-gather.6.cloned.1.call-done), kind=kOutput, calls=%fused_computation.14 | convolution fusion | flops 264095744 | bytes 12821248 | tf_op jit(solution)/shard_map/dot_general | solution.py:30
  145.4 0.0 reduce-scatter.3.cloned.1.call-update
  145.5 91.6 %reduce-scatter.5.cloned.1.call-done = f32[48,2652]{1,0:T(8,128)} async-done(((f32[768,2652]{1,0:T(8,128)}), f32[48,2652]{1,0:T(8,128)}) %reduce-scatter.5.cloned.1.call-update) | async-done | bytes 509200 | tf_op jit(solution)/shard_map/reduce_scatter | solution.py:59
  237.0 1.8 multiply_reduce_fusion.1
  238.8 107.6 %reduce-scatter.3.cloned.1.call-done = f32[48,2704]{1,0:T(8,128)} async-done(((f32[768,2704]{1,0:T(8,128)}), f32[48,2704]{1,0:T(8,128)}) %reduce-scatter.3.cloned.1.call-update) | async-done | bytes 519184 | tf_op jit(solution)/shard_map/reduce_scatter | solution.py:66
  346.4 1.8 multiply_reduce_fusion
  349.5 40.5 %all-reduce = (f32[]{:T(128)}, f32[]{:T(128)}) all-reduce(f32[]{:T(128)S(6)} %add.26, f32[]{:T(128)} %get-tuple-element.6), channel_id=1, replica_groups=mesh['dp'=16,'mp'=2] {'dp','mp'}, use_global_device_ids=true, to_apply=%region_6.7 | all-reduce | flops 2 | bytes 16 | tf_op jit(solution)/shard_map/psum | solution.py:70
  391.4 1.9 broadcast_multiply_fusion.1
  393.3 1.9 broadcast_multiply_fusion
  (2 shorter events, 0.0 us)
Async XLA Ops:
  7.2 56.9 %all-gather.4.cloned.1.call-start = ((), (), s32[]{:S(2)}) async-start(), calls=%async_computation.3 | async-start | bytes 4595712 | tf_op jit(solution)/shard_map/all_gather | solution.py:45
  7.9 107.2 %all-gather.6.cloned.1.call-start = ((), (), s32[]{:S(2)}) async-start(), calls=%async_computation.4 | async-start | bytes 4386816 | tf_op jit(solution)/shard_map/all_gather | solution.py:48
  8.6 228.4 %reduce-scatter.5.cloned.1.call-start = ((), (), s32[]{:S(2)}) async-start(), calls=%async_computation.6 | async-start | bytes 8773632 | tf_op jit(solution)/shard_map/reduce_scatter | solution.py:59
  19.7 105.6 %copy-start = (bf16[16,2652]{1,0:T(8,128)(2,1)S(1)}, bf16[16,2652]{1,0:T(8,128)(2,1)}, u32[]{:S(2)}) copy-start(bf16[16,2652]{1,0:T(8,128)(2,1)} %param.7) | copy-start | bytes 254596
  136.2 210.2 %reduce-scatter.3.cloned.1.call-start = ((), (), s32[]{:S(2)}) async-start(), calls=%async_computation.5 | async-start | bytes 9191424 | tf_op jit(solution)/shard_map/reduce_scatter | solution.py:66
Sparse Core Ops, SparseCore 0:
  10.3 53.7 all-gather.3
  66.4 48.6 all-gather.5
  136.4 100.6 reduce-scatter.4
  241.0 105.4 reduce-scatter.2
where the time goes:
time: 403 us
  waiting for transfers between devices  292 us (72%)
  blocking collectives  63.8 us (16%)
  matrix products  20.1 us (5%)
  between operations  17.6 us (4%)
  other arithmetic  8.71 us (2%)
    reduce_scatter x1, waiting for transfers between devices, body(): lax.psum_scatter(left_product(preact_grad, features), 'dp', scatter_dimen...  108 us
    reduce_scatter x1, waiting for transfers between devices, body(): lax.psum_scatter(left_product(hidden, out_grad), 'dp', scatter_dimension=...  91.6 us
    all_gather x1, waiting for transfers between devices, body(): local_out = lax.all_gather(w_out, 'dp', axis=0, tiled=True)  47.4 us
    all_gather x1, waiting for transfers between devices, body(): local_in = lax.all_gather(w_in, 'dp', axis=0, tiled=True)  44.3 us
    psum x1, blocking collectives, body(): square_total = lax.psum(square_part, ('dp', 'mp'))  40.5 us
    dot_general x2, matrix products, left_product(): lax.dot_general(left_side, right_side, (((0,), (0,)), ((), ())), preferre...  13.6 us
  transfers between devices with their start and end apart: 4, of which 4 were waited for; matrix products, arithmetic and copies ran while one was open for 4% of the time, Pallas kernels for 0%

commit v1 on v0

--- a/solution.py
+++ b/solution.py
@@ -45,7 +45,12 @@
     local_in = lax.all_gather(w_in, "dp", axis=0, tiled=True)
     preact = right_product(features, local_in)
     hidden = jax.nn.gelu(preact).astype(jnp.bfloat16)
-    local_out = lax.all_gather(w_out, "dp", axis=0, tiled=True)
+    ring = [w_out]
+    for hop in range(15):
+        ring.append(lax.ppermute(ring[-1], "dp", [(dev, (dev + 1) % 16) for dev in range(16)]))
+    local_out = jnp.roll(
+        jnp.concatenate(ring[::-1], axis=0), (lax.axis_index("dp") + 1) * ring[0].shape[0], axis=0
+    )
     partial_value = jnp.dot(hidden, local_out, preferred_element_type=jnp.float32)
     stacked = partial_value.astype(jnp.bfloat16).reshape(mp_count, stored_rows, value_width)
     received = lax.all_to_all(stacked, "mp", split_axis=0, concat_axis=0, tiled=True)

time: 403 us -> 470 us (1.17)
  waiting for transfers between devices: 292 us -> 328 us
  local copies, waits for them, and re-layouts: 0.09 us -> 30.3 us
    ppermute x0 -> x15, waiting for transfers between devices: none -> 130 us  [body(): lax.ppermute(ring[-1], 'dp', [(dev, (dev + 1) % 16) for dev in range(16)])]
    all_gather x1, waiting for transfers between devices: 47.4 us -> 0.02 us  [body(): back_out = lax.all_gather(w_out, 'dp', axis=0, tiled=True)]
    all_gather x1, waiting for transfers between devices: 44.3 us -> 0.01 us  [body(): local_in = lax.all_gather(w_in, 'dp', axis=0, tiled=True)]
    unnamed x3 -> x44, local copies, waits for them, and re-layouts: 0.09 us -> 29.5 us
  transfers between devices with their start and end apart: 4 -> 19, of which waited for: 4 -> 16; matrix products, arithmetic and copies ran while one was open for 4% -> 11% of each run, Pallas kernels for 0% -> 0%
where the time goes in v1:
time: 470 us; the launch traced here: 469 us
  waiting for transfers between devices  328 us (70%)
  blocking collectives  62.9 us (13%)
  local copies, waits for them, and re-layouts  30.3 us (6%)
  matrix products  21 us (4%)
  between operations  17.6 us (4%)
  other arithmetic  8.71 us (2%)
    ppermute x15, waiting for transfers between devices, body(): lax.ppermute(ring[-1], 'dp', [(dev, (dev + 1) % 16) for dev in range(16)])  130 us
    reduce_scatter x1, waiting for transfers between devices, body(): lax.psum_scatter(left_product(preact_grad, features), 'dp', scatter_dimen...  108 us
    reduce_scatter x1, waiting for transfers between devices, body(): lax.psum_scatter(left_product(hidden, out_grad), 'dp', scatter_dimension=...  89.4 us
    psum x1, blocking collectives, body(): square_total = lax.psum(square_part, ('dp', 'mp'))  40.5 us
    unnamed x44, local copies, waits for them, and re-layouts  29.5 us
    dot_general x2, matrix products, left_product(): lax.dot_general(left_side, right_side, (((0,), (0,)), ((), ())), preferre...  14 us
  transfers between devices with their start and end apart: 19, of which 16 were waited for; matrix products, arithmetic and copies ran while one was open for 11% of the time, Pallas kernels for 0%

profile of v1, /device:TPU:0, one launch (start us, length us, event | category | flops | bytes accessed | tf_op | source)
XLA Modules:
  0.0 468.9 jit_solution(7050164687897728553)
XLA Ops:
  8.5 9.2 %collective-permute-done = bf16[48,2652]{1,0:T(8,128)(2,1)S(1)} collective-permute-done((bf16[48,2652]{1,0:T(8,128)(2,1)}, bf16[48,2652]{1,0:T(8,128)(2,1)S(1)}, u32[]{:S(2)}, u32[]{:S(2)}) %collective-permute-start) | collective-permute-done | bytes 254624 | tf_op jit(solution)/shard_map/ppermute | solution.py:50
  17.7 8.6 %collective-permute-done.1 = bf16[48,2652]{1,0:T(8,128)(2,1)S(1)} collective-permute-done((bf16[48,2652]{1,0:T(8,128)(2,1)S(1)}, bf16[48,2652]{1,0:T(8,128)(2,1)S(1)}, u32[]{:S(2)}, u32[]{:S(2)}) %collective-permute-start.1) | collective-permute-done | bytes 254624 | tf_op jit(solution)/shard_map/ppermute | solution.py:50
  26.3 11.8 %collective-permute-done.2 = bf16[48,2652]{1,0:T(8,128)(2,1)S(1)} collective-permute-done((bf16[48,2652]{1,0:T(8,128)(2,1)S(1)}, bf16[48,2652]{1,0:T(8,128)(2,1)S(1)}, u32[]{:S(2)}, u32[]{:S(2)}) %collective-permute-start.2) | collective-permute-done | bytes 254624 | tf_op jit(solution)/shard_map/ppermute | solution.py:50
  38.0 9.1 %collective-permute-done.3 = bf16[48,2652]{1,0:T(8,128)(2,1)S(1)} collective-permute-done((bf16[48,2652]{1,0:T(8,128)(2,1)S(1)}, bf16[48,2652]{1,0:T(8,128)(2,1)S(1)}, u32[]{:S(2)}, u32[]{:S(2)}) %collective-permute-start.3) | collective-permute-done | bytes 254624 | tf_op jit(solution)/shard_map/ppermute | solution.py:50
  47.1 13.2 %collective-permute-done.4 = bf16[48,2652]{1,0:T(8,128)(2,1)S(1)} collective-permute-done((bf16[48,2652]{1,0:T(8,128)(2,1)S(1)}, bf16[48,2652]{1,0:T(8,128)(2,1)S(1)}, u32[]{:S(2)}, u32[]{:S(2)}) %collective-permute-start.4) | collective-permute-done | bytes 254624 | tf_op jit(solution)/shard_map/ppermute | solution.py:50
  60.4 10.2 %collective-permute-done.5 = bf16[48,2652]{1,0:T(8,128)(2,1)S(1)} collective-permute-done((bf16[48,2652]{1,0:T(8,128)(2,1)S(1)}, bf16[48,2652]{1,0:T(8,128)(2,1)S(1)}, u32[]{:S(2)}, u32[]{:S(2)}) %collective-permute-start.5) | collective-permute-done | bytes 254624 | tf_op jit(solution)/shard_map/ppermute | solution.py:50
  70.6 8.4 %collective-permute-done.6 = bf16[48,2652]{1,0:T(8,128)(2,1)S(1)} collective-permute-done((bf16[48,2652]{1,0:T(8,128)(2,1)S(1)}, bf16[48,2652]{1,0:T(8,128)(2,1)S(1)}, u32[]{:S(2)}, u32[]{:S(2)}) %collective-permute-start.6) | collective-permute-done | bytes 254624 | tf_op jit(solution)/shard_map/ppermute | solution.py:50
  79.1 8.4 %collective-permute-done.7 = bf16[48,2652]{1,0:T(8,128)(2,1)S(1)} collective-permute-done((bf16[48,2652]{1,0:T(8,128)(2,1)S(1)}, bf16[48,2652]{1,0:T(8,128)(2,1)S(1)}, u32[]{:S(2)}, u32[]{:S(2)}) %collective-permute-start.7) | collective-permute-done | bytes 254624 | tf_op jit(solution)/shard_map/ppermute | solution.py:50
  87.5 8.4 %collective-permute-done.8 = bf16[48,2652]{1,0:T(8,128)(2,1)S(1)} collective-permute-done((bf16[48,2652]{1,0:T(8,128)(2,1)S(1)}, bf16[48,2652]{1,0:T(8,128)(2,1)S(1)}, u32[]{:S(2)}, u32[]{:S(2)}) %collective-permute-start.8) | collective-permute-done | bytes 254624 | tf_op jit(solution)/shard_map/ppermute | solution.py:50
  96.0 8.4 %collective-permute-done.9 = bf16[48,2652]{1,0:T(8,128)(2,1)S(1)} collective-permute-done((bf16[48,2652]{1,0:T(8,128)(2,1)S(1)}, bf16[48,2652]{1,0:T(8,128)(2,1)S(1)}, u32[]{:S(2)}, u32[]{:S(2)}) %collective-permute-start.9) | collective-permute-done | bytes 254624 | tf_op jit(solution)/shard_map/ppermute | solution.py:50
  104.4 8.4 %collective-permute-done.10 = bf16[48,2652]{1,0:T(8,128)(2,1)S(1)} collective-permute-done((bf16[48,2652]{1,0:T(8,128)(2,1)S(1)}, bf16[48,2652]{1,0:T(8,128)(2,1)S(1)}, u32[]{:S(2)}, u32[]{:S(2)}) %collective-permute-start.10) | collective-permute-done | bytes 254624 | tf_op jit(solution)/shard_map/ppermute | solution.py:50
  112.9 8.4 %collective-permute-done.11 = bf16[48,2652]{1,0:T(8,128)(2,1)S(1)} collective-permute-done((bf16[48,2652]{1,0:T(8,128)(2,1)S(1)}, bf16[48,2652]{1,0:T(8,128)(2,1)S(1)}, u32[]{:S(2)}, u32[]{:S(2)}) %collective-permute-start.11) | collective-permute-done | bytes 254624 | tf_op jit(solution)/shard_map/ppermute | solution.py:50
  121.3 0.7 copy-done.1
  122.0 8.4 %collective-permute-done.12 = bf16[48,2652]{1,0:T(8,128)(2,1)S(1)} collective-permute-done((bf16[48,2652]{1,0:T(8,128)(2,1)S(1)}, bf16[48,2652]{1,0:T(8,128)(2,1)S(1)}, u32[]{:S(2)}, u32[]{:S(2)}) %collective-permute-start.12) | collective-permute-done | bytes 254624 | tf_op jit(solution)/shard_map/ppermute | solution.py:50
  130.5 0.7 copy-done.3
  131.2 8.6 %collective-permute-done.13 = bf16[48,2652]{1,0:T(8,128)(2,1)} collective-permute-done((bf16[48,2652]{1,0:T(8,128)(2,1)S(1)}, bf16[48,2652]{1,0:T(8,128)(2,1)}, u32[]{:S(2)}, u32[]{:S(2)}) %collective-permute-start.13) | collective-permute-done | bytes 254624 | tf_op jit(solution)/shard_map/ppermute | solution.py:50
  139.8 4.5 all-gather
  144.4 5.5 %all_gather.15 = bf16[32,2652]{1,0:T(8,128)(2,1)S(1)} all-gather(bf16[16,2652]{1,0:T(8,128)(2,1)} %param.5), channel_id=1, replica_groups=mesh['dp'=16,'mp'=2] {'mp'}, dimensions={0}, use_global_device_ids=true | all-gather | bytes 254592 | tf_op jit(solution)/shard_map/all_gather | solution.py:41
  150.0 1.7 constant_dynamic-update-slice_fusion.31
  151.7 1.7 constant_dynamic-update-slice_fusion.30
  153.3 1.7 constant_dynamic-update-slice_fusion.29
  155.0 1.7 constant_dynamic-update-slice_fusion.28
  156.7 0.7 constant_dynamic-update-slice_fusion.27
  157.4 0.7 constant_dynamic-update-slice_fusion.26
  158.1 0.7 constant_dynamic-update-slice_fusion.25
  158.8 0.7 constant_dynamic-update-slice_fusion.24
  159.5 0.7 constant_dynamic-update-slice_fusion.23
  160.3 0.7 constant_dynamic-update-slice_fusion.22
  161.0 0.7 constant_dynamic-update-slice_fusion.21
  161.7 0.7 constant_dynamic-update-slice_fusion.20
  162.4 0.7 constant_dynamic-update-slice_fusion.19
  163.1 0.7 constant_dynamic-update-slice_fusion.18
  163.9 0.7 constant_dynamic-update-slice_fusion.17
  164.6 0.7 constant_dynamic-update-slice_fusion.16
  165.3 1.7 constant_dynamic-update-slice_fusion.15
  166.9 1.7 constant_dynamic-update-slice_fusion.14
  168.6 0.7 constant_dynamic-update-slice_fusion.13
  169.4 0.7 constant_dynamic-update-slice_fusion.12
  170.1 0.7 constant_dynamic-update-slice_fusion.11
  170.8 0.7 constant_dynamic-update-slice_fusion.10
  171.6 0.7 constant_dynamic-update-slice_fusion.9
  172.3 0.7 constant_dynamic-update-slice_fusion.8
  173.0 0.7 constant_dynamic-update-slice_fusion.7
  173.7 0.7 constant_dynamic-update-slice_fusion.6
  174.4 0.7 constant_dynamic-update-slice_fusion.5
  175.1 0.7 constant_dynamic-update-slice_fusion.4
  175.9 0.7 constant_dynamic-update-slice_fusion.3
  176.6 0.7 constant_dynamic-update-slice_fusion.2
  177.3 0.7 constant_dynamic-update-slice_fusion.1
  178.0 0.8 constant_dynamic-update-slice_fusion
  178.8 3.6 fusion.8
  182.4 3.5 fusion.2
  185.9 7.2 %all_to_all.5 = bf16[2,16,2652]{2,1,0:T(8,128)(2,1)S(1)} all-to-all(bf16[2,16,2652]{2,1,0:T(8,128)(2,1)S(1)} %bitcast.8), channel_id=1, replica_groups=mesh['dp'=16,'mp'=2] {'mp'}, dimensions={0} | all-to-all | bytes 339456 | tf_op jit(solution)/shard_map/all_to_all | solution.py:56
  193.2 1.3 fusion.6
  194.4 5.1 %all_gather.18 = bf16[32,2652]{1,0:T(8,128)(2,1)S(1)} all-gather(bf16[16,2652]{1,0:T(8,128)(2,1)S(1)} %get-tuple-element.7), channel_id=1, replica_groups=mesh['dp'=16,'mp'=2] {'mp'}, dimensions={0}, use_global_device_ids=true | all-gather | bytes 254592 | tf_op jit(solution)/shard_map/all_gather | solution.py:60
  199.6 4.5 fusion.32
  204.2 9.5 %fusion.7 = f32[768,2704]{1,0:T(8,128)} fusion(bf16[32,52]{1,0:T(8,128)(2,1)S(1)} %convert_reduce_fusion.1, bf16[32,2652]{1,0:T(8,128)(2,1)S(1)} %all_gather.15, f32[32,768]{1,0:T(8,128)S(1)} %fusion.8, bf16[32,2652]{1,0:T(8,128)(2,1)S(1)} %all_gather.18, bf16[768,2652]{1,0:T(8,128)(2,1)} %all-gather.6.cloned.1.call-done), kind=kOutput, calls=%fused_computation.16 | convolution fusion | flops 264095744 | bytes 12821248 | tf_op jit(solution)/shard_map/dot_general | solution.py:30
  213.7 89.4 %reduce-scatter.5.cloned.1.call-done = f32[48,2652]{1,0:T(8,128)} async-done(((f32[768,2652]{1,0:T(8,128)}), f32[48,2652]{1,0:T(8,128)}) %reduce-scatter.5.cloned.1.call-update) | async-done | bytes 509200 | tf_op jit(solution)/shard_map/reduce_scatter | solution.py:64
  303.1 1.8 multiply_reduce_fusion.1
  304.9 107.7 %reduce-scatter.3.cloned.1.call-done = f32[48,2704]{1,0:T(8,128)} async-done(((f32[768,2704]{1,0:T(8,128)}), f32[48,2704]{1,0:T(8,128)}) %reduce-scatter.3.cloned.1.call-update) | async-done | bytes 519184 | tf_op jit(solution)/shard_map/reduce_scatter | solution.py:71
  412.5 1.8 multiply_reduce_fusion
  415.6 40.5 %all-reduce = (f32[]{:T(128)}, f32[]{:T(128)}) all-reduce(f32[]{:T(128)S(6)} %add.42, f32[]{:T(128)} %get-tuple-element.6), channel_id=1, replica_groups=mesh['dp'=16,'mp'=2] {'dp','mp'}, use_global_device_ids=true, to_apply=%region_6.7 | all-reduce | flops 2 | bytes 16 | tf_op jit(solution)/shard_map/psum | solution.py:75
  457.5 1.9 broadcast_multiply_fusion.1
  459.4 1.9 broadcast_multiply_fusion
  (40 shorter events, 1.7 us)
Async XLA Ops:
  7.2 157.4 %copy-start = (bf16[48,2652]{1,0:T(8,128)(2,1)S(1)}, bf16[48,2652]{1,0:T(8,128)(2,1)}, u32[]{:S(2)}) copy-start(bf16[48,2652]{1,0:T(8,128)(2,1)} %param.9) | copy-start | bytes 763780
  7.2 171.6 %all-gather.4.cloned.1.call-start = ((), (), s32[]{:S(2)}) async-start(), calls=%async_computation.3 | async-start | bytes 4595712 | tf_op jit(solution)/shard_map/all_gather | solution.py:45
  7.9 196.3 %all-gather.6.cloned.1.call-start = ((), (), s32[]{:S(2)}) async-start(), calls=%async_computation.4 | async-start | bytes 4386816 | tf_op jit(solution)/shard_map/all_gather | solution.py:67
  8.0 9.7 %collective-permute-start = (bf16[48,2652]{1,0:T(8,128)(2,1)}, bf16[48,2652]{1,0:T(8,128)(2,1)S(1)}, u32[]{:S(2)}, u32[]{:S(2)}) collective-permute-start(bf16[48,2652]{1,0:T(8,128)(2,1)} %param.9), channel_id=1, source_target_pairs={{0,2},{2,4},{4,6},{6,8},{8,10},{10,12},{12,14},{14,16},{16,18},{18... | collective-permute-start | bytes 763784 | tf_op jit(solution)/shard_map/ppermute | solution.py:50
  17.7 8.6 %collective-permute-start.1 = (bf16[48,2652]{1,0:T(8,128)(2,1)S(1)}, bf16[48,2652]{1,0:T(8,128)(2,1)S(1)}, u32[]{:S(2)}, u32[]{:S(2)}) collective-permute-start(bf16[48,2652]{1,0:T(8,128)(2,1)S(1)} %collective-permute-done), channel_id=1, source_target_pairs={{0,2},{2,4},{4,6},{6,8},{8,10},{10,12},{12,14},{14,16},{16,18},{18... | collective-permute-start | bytes 763784 | tf_op jit(solution)/shard_map/ppermute | solution.py:50
  26.3 11.8 %collective-permute-start.2 = (bf16[48,2652]{1,0:T(8,128)(2,1)S(1)}, bf16[48,2652]{1,0:T(8,128)(2,1)S(1)}, u32[]{:S(2)}, u32[]{:S(2)}) collective-permute-start(bf16[48,2652]{1,0:T(8,128)(2,1)S(1)} %collective-permute-done.1), channel_id=1, source_target_pairs={{0,2},{2,4},{4,6},{6,8},{8,10},{10,12},{12,14},{14,16},{16,18},{18... | collective-permute-start | bytes 763784 | tf_op jit(solution)/shard_map/ppermute | solution.py:50
  38.0 9.1 %collective-permute-start.3 = (bf16[48,2652]{1,0:T(8,128)(2,1)S(1)}, bf16[48,2652]{1,0:T(8,128)(2,1)S(1)}, u32[]{:S(2)}, u32[]{:S(2)}) collective-permute-start(bf16[48,2652]{1,0:T(8,128)(2,1)S(1)} %collective-permute-done.2), channel_id=1, source_target_pairs={{0,2},{2,4},{4,6},{6,8},{8,10},{10,12},{12,14},{14,16},{16,18},{18... | collective-permute-start | bytes 763784 | tf_op jit(solution)/shard_map/ppermute | solution.py:50
  47.1 13.2 %collective-permute-start.4 = (bf16[48,2652]{1,0:T(8,128)(2,1)S(1)}, bf16[48,2652]{1,0:T(8,128)(2,1)S(1)}, u32[]{:S(2)}, u32[]{:S(2)}) collective-permute-start(bf16[48,2652]{1,0:T(8,128)(2,1)S(1)} %collective-permute-done.3), channel_id=1, source_target_pairs={{0,2},{2,4},{4,6},{6,8},{8,10},{10,12},{12,14},{14,16},{16,18},{18... | collective-permute-start | bytes 763784 | tf_op jit(solution)/shard_map/ppermute | solution.py:50
  60.4 10.2 %collective-permute-start.5 = (bf16[48,2652]{1,0:T(8,128)(2,1)S(1)}, bf16[48,2652]{1,0:T(8,128)(2,1)S(1)}, u32[]{:S(2)}, u32[]{:S(2)}) collective-permute-start(bf16[48,2652]{1,0:T(8,128)(2,1)S(1)} %collective-permute-done.4), channel_id=1, source_target_pairs={{0,2},{2,4},{4,6},{6,8},{8,10},{10,12},{12,14},{14,16},{16,18},{18... | collective-permute-start | bytes 763784 | tf_op jit(solution)/shard_map/ppermute | solution.py:50
  70.6 8.5 %collective-permute-start.6 = (bf16[48,2652]{1,0:T(8,128)(2,1)S(1)}, bf16[48,2652]{1,0:T(8,128)(2,1)S(1)}, u32[]{:S(2)}, u32[]{:S(2)}) collective-permute-start(bf16[48,2652]{1,0:T(8,128)(2,1)S(1)} %collective-permute-done.5), channel_id=1, source_target_pairs={{0,2},{2,4},{4,6},{6,8},{8,10},{10,12},{12,14},{14,16},{16,18},{18... | collective-permute-start | bytes 763784 | tf_op jit(solution)/shard_map/ppermute | solution.py:50
  79.1 8.5 %collective-permute-start.7 = (bf16[48,2652]{1,0:T(8,128)(2,1)S(1)}, bf16[48,2652]{1,0:T(8,128)(2,1)S(1)}, u32[]{:S(2)}, u32[]{:S(2)}) collective-permute-start(bf16[48,2652]{1,0:T(8,128)(2,1)S(1)} %collective-permute-done.6), channel_id=1, source_target_pairs={{0,2},{2,4},{4,6},{6,8},{8,10},{10,12},{12,14},{14,16},{16,18},{18... | collective-permute-start | bytes 763784 | tf_op jit(solution)/shard_map/ppermute | solution.py:50
  87.5 8.5 %collective-permute-start.8 = (bf16[48,2652]{1,0:T(8,128)(2,1)S(1)}, bf16[48,2652]{1,0:T(8,128)(2,1)S(1)}, u32[]{:S(2)}, u32[]{:S(2)}) collective-permute-start(bf16[48,2652]{1,0:T(8,128)(2,1)S(1)} %collective-permute-done.7), channel_id=1, source_target_pairs={{0,2},{2,4},{4,6},{6,8},{8,10},{10,12},{12,14},{14,16},{16,18},{18... | collective-permute-start | bytes 763784 | tf_op jit(solution)/shard_map/ppermute | solution.py:50
  96.0 8.5 %collective-permute-start.9 = (bf16[48,2652]{1,0:T(8,128)(2,1)S(1)}, bf16[48,2652]{1,0:T(8,128)(2,1)S(1)}, u32[]{:S(2)}, u32[]{:S(2)}) collective-permute-start(bf16[48,2652]{1,0:T(8,128)(2,1)S(1)} %collective-permute-done.8), channel_id=1, source_target_pairs={{0,2},{2,4},{4,6},{6,8},{8,10},{10,12},{12,14},{14,16},{16,18},{18... | collective-permute-start | bytes 763784 | tf_op jit(solution)/shard_map/ppermute | solution.py:50
  104.4 8.5 %collective-permute-start.10 = (bf16[48,2652]{1,0:T(8,128)(2,1)S(1)}, bf16[48,2652]{1,0:T(8,128)(2,1)S(1)}, u32[]{:S(2)}, u32[]{:S(2)}) collective-permute-start(bf16[48,2652]{1,0:T(8,128)(2,1)S(1)} %collective-permute-done.9), channel_id=1, source_target_pairs={{0,2},{2,4},{4,6},{6,8},{8,10},{10,12},{12,14},{14,16},{16,18},{18... | collective-permute-start | bytes 763784 | tf_op jit(solution)/shard_map/ppermute | solution.py:50
  112.9 8.5 %collective-permute-start.11 = (bf16[48,2652]{1,0:T(8,128)(2,1)S(1)}, bf16[48,2652]{1,0:T(8,128)(2,1)S(1)}, u32[]{:S(2)}, u32[]{:S(2)}) collective-permute-start(bf16[48,2652]{1,0:T(8,128)(2,1)S(1)} %collective-permute-done.10), channel_id=1, source_target_pairs={{0,2},{2,4},{4,6},{6,8},{8,10},{10,12},{12,14},{14,16},{16,18},{18... | collective-permute-start | bytes 763784 | tf_op jit(solution)/shard_map/ppermute | solution.py:50
  121.3 0.7 copy-start.1
  122.0 8.5 %collective-permute-start.12 = (bf16[48,2652]{1,0:T(8,128)(2,1)S(1)}, bf16[48,2652]{1,0:T(8,128)(2,1)S(1)}, u32[]{:S(2)}, u32[]{:S(2)}) collective-permute-start(bf16[48,2652]{1,0:T(8,128)(2,1)S(1)} %collective-permute-done.11), channel_id=1, source_target_pairs={{0,2},{2,4},{4,6},{6,8},{8,10},{10,12},{12,14},{14,16},{16,18},{18... | collective-permute-start | bytes 763784 | tf_op jit(solution)/shard_map/ppermute | solution.py:50
  130.5 0.7 copy-start.3
  131.2 8.6 %collective-permute-start.13 = (bf16[48,2652]{1,0:T(8,128)(2,1)S(1)}, bf16[48,2652]{1,0:T(8,128)(2,1)}, u32[]{:S(2)}, u32[]{:S(2)}) collective-permute-start(bf16[48,2652]{1,0:T(8,128)(2,1)S(1)} %collective-permute-done.12), channel_id=1, source_target_pairs={{0,2},{2,4},{4,6},{6,8},{8,10},{10,12},{12,14},{14,16},{16,18},{18... | collective-permute-start | bytes 763784 | tf_op jit(solution)/shard_map/ppermute | solution.py:50
  139.7 10.3 %collective-permute-start.14 = (bf16[48,2652]{1,0:T(8,128)(2,1)}, bf16[48,2652]{1,0:T(8,128)(2,1)}, u32[]{:S(2)}, u32[]{:S(2)}) collective-permute-start(bf16[48,2652]{1,0:T(8,128)(2,1)} %collective-permute-done.13), channel_id=1, source_target_pairs={{0,2},{2,4},{4,6},{6,8},{8,10},{10,12},{12,14},{14,16},{16,18},{18... | collective-permute-start | bytes 763784 | tf_op jit(solution)/shard_map/ppermute | solution.py:50
  139.7 163.4 %reduce-scatter.5.cloned.1.call-start = ((), (), s32[]{:S(2)}) async-start(), calls=%async_computation.6 | async-start | bytes 8773632 | tf_op jit(solution)/shard_map/reduce_scatter | solution.py:64
  144.4 24.2 %copy-start.4 = (bf16[48,2652]{1,0:T(8,128)(2,1)S(1)}, bf16[48,2652]{1,0:T(8,128)(2,1)}, u32[]{:S(2)}) copy-start(bf16[48,2652]{1,0:T(8,128)(2,1)} %copy-done.3) | copy-start | bytes 763780
  144.4 25.0 %copy-start.2 = (bf16[48,2652]{1,0:T(8,128)(2,1)S(1)}, bf16[48,2652]{1,0:T(8,128)(2,1)}, u32[]{:S(2)}) copy-start(bf16[48,2652]{1,0:T(8,128)(2,1)} %copy-done.1) | copy-start | bytes 763780
  169.4 23.8 %copy-start.5 = (bf16[16,2652]{1,0:T(8,128)(2,1)S(1)}, bf16[16,2652]{1,0:T(8,128)(2,1)}, u32[]{:S(2)}) copy-start(bf16[16,2652]{1,0:T(8,128)(2,1)} %param.7) | copy-start | bytes 254596
  204.1 208.4 %reduce-scatter.3.cloned.1.call-start = ((), (), s32[]{:S(2)}) async-start(), calls=%async_computation.5 | async-start | bytes 9191424 | tf_op jit(solution)/shard_map/reduce_scatter | solution.py:71
Sparse Core Ops, SparseCore 0:
  10.3 58.3 all-gather.3
  139.9 51.2 all-gather.5
  204.2 98.8 reduce-scatter.4
  307.0 105.4 reduce-scatter.2
